TPU v7x, 32 devices: a whole 2x2x4 slice. The times are simulated.
32 devices in a mesh: section: 4 (over y, x), expert: 8 (over z, core).
Axes of the slice: x: 2, y: 2, z: 4, core: 2. Of those that a mesh axis runs over, the one named last changes fastest.
Arguments:
- tokens: bfloat16 [8, 64, 2048], P(None, 'expert'), may hold values from -6 to 6
- norm_gain: float32 [2, 2048], replicated, may hold values from 0.1 to 1.9
- w_gate: bfloat16 [4, 2048, 14336], P('section', None, 'expert'), may hold values from -0.125 to 0.125
- w_up: bfloat16 [4, 2048, 14336], P('section', None, 'expert'), may hold values from -0.125 to 0.125
- w_down: bfloat16 [4, 14336, 2048], P('section', 'expert'), may hold values from -0.0625 to 0.0625
- expert_ids: int32 [2, 8, 64, 2], P(None, None, 'expert'), may hold values from 0 to 3, as said below
- slot_ids: int32 [2, 8, 64, 2], P(None, None, 'expert'), may hold values from 0 to 4, as said below
- dropped: int32 [2, 8, 64, 2], P(None, None, 'expert'), may hold values from 0 to 1, as said below
- gate_weights: float32 [2, 8, 64, 2], P(None, None, 'expert'), may hold values from 0.1 to 1
Outputs:
- states: bfloat16 [4, 8, 64, 2048], P('section', None, 'expert')
Inputs may be any that keep to these rules, and one draw needn't show every extreme that they name: `expert_ids`: the two experts of a token differ. `slot_ids`: among the kept choices of the tokens of one index of expert that name one expert, the slots are 0, 1, ... up to their count less one, each once. At most 5 kept choices of the tokens of one index of expert name one expert, and a choice is dropped only where 5 kept choices of its index of expert name its expert; in each layer and micro-batch some expert receives exactly 5 kept choices from every index of expert.
All inputs are finite; a program needn't handle non-finite values.
Results may differ from a plain program's by a relative error of at most 0.025.
Values may be sent and summed in bfloat16 or wider, within the bound.
A program may use at most 64 MiB of HBM per device.

v0:
```python
import jax
import jax.numpy as jnp
from jax import lax
from jax.sharding import PartitionSpec as P

EXPERTS = 4


def shortened(value):
    return jax.tree.map(lambda a: a.astype(jnp.bfloat16) if a.dtype == jnp.float32 else a, value)


def shifted(value, axis, by):
    size = lax.axis_size(axis)
    pairs = [(i, i + by) for i in range(size) if 0 <= i + by < size]
    return lax.ppermute(value, axis, pairs)


def on_device(tokens, norm_gain, w_gate, w_up, w_down, expert_ids, slot_ids, dropped, gate_weights):
    groups = lax.axis_size("expert")
    sections = lax.axis_size("section")
    section_at = lax.axis_index("section")
    local_count = EXPERTS // 2
    shards = groups // local_count
    micro_count, tok_rows, model_width = tokens.shape
    capacity = 5 * tok_rows // (2 * EXPERTS)
    slot_limit = local_count * capacity
    layer_at = section_at // 2
    half_at = section_at % 2
    odd_section = half_at == 1
    gain_row = lax.dynamic_index_in_dim(norm_gain, layer_at, 0, keepdims=False)
    gate_mat = w_gate[0]
    up_mat = w_up[0]
    down_mat = w_down[0]
    route_all = lax.dynamic_index_in_dim(expert_ids, layer_at, 0, keepdims=False)
    slot_all = lax.dynamic_index_in_dim(slot_ids, layer_at, 0, keepdims=False)
    drop_all = lax.dynamic_index_in_dim(dropped, layer_at, 0, keepdims=False)
    weigh_all = lax.dynamic_index_in_dim(gate_weights, layer_at, 0, keepdims=False)

    def expert_rows(received):
        flat_rows = received.reshape(-1, model_width)
        gate_vals = jnp.dot(flat_rows, gate_mat, preferred_element_type=jnp.float32)
        up_vals = jnp.dot(flat_rows, up_mat, preferred_element_type=jnp.float32)
        hidden = (jax.nn.silu(gate_vals) * up_vals).astype(jnp.bfloat16)
        partial_rows = jnp.dot(hidden, down_mat, preferred_element_type=jnp.float32).astype(
            jnp.bfloat16
        )
        return partial_rows.reshape(received.shape)

    def skip_rows(received):
        return jnp.zeros(received.shape, jnp.bfloat16)

    def run_experts(outgoing, active):
        received = lax.all_to_all(outgoing, "expert", split_axis=0, concat_axis=0, tiled=True)
        computed = lax.cond(active, expert_rows, skip_rows, received)
        returned = lax.all_to_all(computed, "expert", split_axis=0, concat_axis=0, tiled=True)
        return returned

    def advance(tick_count, carry):
        incoming, states = carry
        micro_at = tick_count - section_at
        active = (micro_at >= 0) & (micro_at < micro_count)
        micro_index = jnp.clip(micro_at, 0, micro_count - 1)
        fresh_rows = lax.dynamic_index_in_dim(tokens, micro_index, 0, keepdims=False)
        route_now = lax.dynamic_index_in_dim(route_all, micro_index, 0, keepdims=False)
        slot_now = lax.dynamic_index_in_dim(slot_all, micro_index, 0, keepdims=False)
        drop_now = lax.dynamic_index_in_dim(drop_all, micro_index, 0, keepdims=False)
        weigh_now = lax.dynamic_index_in_dim(weigh_all, micro_index, 0, keepdims=False)
        kept_mask = drop_now == 0
        passed_state = incoming[0]
        prior_rows = [incoming[1], incoming[2]]
        current = jnp.where(section_at == 0, fresh_rows, passed_state)
        wide_rows = current.astype(jnp.float32)
        inv_scale = lax.rsqrt(jnp.mean(wide_rows * wide_rows, axis=-1, keepdims=True) + 1e-05)
        normed = (wide_rows * inv_scale * gain_row).astype(jnp.bfloat16)
        local_id = route_now - half_at * local_count
        owned = kept_mask & (local_id >= 0) & (local_id < local_count)
        target = jnp.where(owned, local_id * capacity + slot_now, slot_limit)
        buffer = jnp.zeros((slot_limit, model_width), jnp.bfloat16)
        buffer = buffer.at[target[:, 0]].set(normed, mode="drop")
        buffer = buffer.at[target[:, 1]].set(normed, mode="drop")
        buffer = buffer.reshape(local_count, capacity, model_width)
        outgoing = jnp.repeat(buffer, shards, axis=0)
        returned = run_experts(outgoing, active)
        summed = jnp.sum(
            returned.astype(jnp.float32).reshape(local_count, shards, capacity, model_width), axis=1
        )
        flat_back = summed.astype(jnp.bfloat16).reshape(slot_limit, model_width)
        clipped = jnp.minimum(target, slot_limit - 1)
        combined = wide_rows
        chosen_rows = []
        for member in range(2):
            own_rows = flat_back[clipped[:, member]]
            chosen = jnp.where(owned[:, member : member + 1], own_rows, prior_rows[member])
            chosen_rows.append(chosen)
            combined = combined + weigh_now[:, member : member + 1] * chosen.astype(jnp.float32)
        mixed_rows = combined.astype(jnp.bfloat16)
        updated = lax.dynamic_update_index_in_dim(states, mixed_rows, micro_index, 0)
        states = jnp.where(active, updated, states)
        zero_rows = jnp.zeros_like(current)
        even_load = jnp.stack([current, chosen_rows[0], chosen_rows[1]])
        odd_load = jnp.stack([mixed_rows, zero_rows, zero_rows])
        payload = jnp.where(odd_section, odd_load, even_load)
        passed = shifted(shortened(payload), "section", 1).astype(payload.dtype)
        return (passed, states)

    start_load = jnp.zeros((3, tok_rows, model_width), jnp.bfloat16)
    initial = (start_load, jnp.zeros((micro_count, tok_rows, model_width), jnp.bfloat16))
    final_load, states = lax.fori_loop(0, micro_count + sections - 1, advance, initial)
    return states[None]


def solution(mesh):
    return jax.shard_map(
        on_device,
        mesh=mesh,
        in_specs=(
            P(None, "expert", None),
            P(),
            P("section", None, "expert"),
            P("section", None, "expert"),
            P("section", "expert", None),
            P(None, None, "expert", None),
            P(None, None, "expert", None),
            P(None, None, "expert", None),
            P(None, None, "expert", None),
        ),
        out_specs=P("section", None, "expert", None),
        check_vma=False,
    )
```

profile of v0, /device:TPU:6, one launch (start us, length us, event | category | flops | bytes accessed | tf_op | source)
XLA Modules:
  0.0 560.5 jit_solution(8104722328637122049)
XLA Ops:
  2.2 557.6 %while.17 = (s32[]{:T(128)}, bf16[3,8,2048]{2,1,0:T(8,128)(2,1)S(1)}, bf16[8,8,2048]{2,1,0:T(8,128)(2,1)S(1)}, pred[]{:T(512)}, pred[]{:T(512)}, /*index=5*/s32[...) while((s32[]{:T(128)}, ...), condition=%wide.region_7.8_spmd, body=%wide.region_0.7_spmd.sunk | while | flops 881903936 | bytes 27046772 | solution.py:109
  10.4 9.7 %all-to-all-done = bf16[8,5,2048]{2,1,0:T(8,128)(2,1)S(1)} async-done(((bf16[8,5,2048]{2,1,0:T(8,128)(2,1)}), bf16[8,5,2048]{2,1,0:T(8,128)(2,1)S(1)}, u32[]{:S(2)}, u32[]{:S(2)}) %all-to-all-start) | async-done | bytes 163872 | tf_op jit(solution)/shard_map/while/body/eval_jaxpr/all_to_all | solution.py:54
  24.3 9.6 %all-to-all-done.1 = bf16[8,5,2048]{2,1,0:T(8,128)(2,1)S(1)} async-done(((bf16[8,5,2048]{2,1,0:T(8,128)(2,1)}), bf16[8,5,2048]{2,1,0:T(8,128)(2,1)S(1)}, u32[]{:S(2)}, u32[]{:S(2)}) %all-to-all-start.1) | async-done | bytes 163872 | tf_op jit(solution)/shard_map/while/body/eval_jaxpr/all_to_all | solution.py:56
  48.5 9.6 %all-to-all-done = bf16[8,5,2048]{2,1,0:T(8,128)(2,1)S(1)} async-done(((bf16[8,5,2048]{2,1,0:T(8,128)(2,1)}), bf16[8,5,2048]{2,1,0:T(8,128)(2,1)S(1)}, u32[]{:S(2)}, u32[]{:S(2)}) %all-to-all-start) | async-done | bytes 163872 | tf_op jit(solution)/shard_map/while/body/eval_jaxpr/all_to_all | solution.py:54
  62.3 9.6 %all-to-all-done.1 = bf16[8,5,2048]{2,1,0:T(8,128)(2,1)S(1)} async-done(((bf16[8,5,2048]{2,1,0:T(8,128)(2,1)}), bf16[8,5,2048]{2,1,0:T(8,128)(2,1)S(1)}, u32[]{:S(2)}, u32[]{:S(2)}) %all-to-all-start.1) | async-done | bytes 163872 | tf_op jit(solution)/shard_map/while/body/eval_jaxpr/all_to_all | solution.py:56
  86.5 9.6 %all-to-all-done = bf16[8,5,2048]{2,1,0:T(8,128)(2,1)S(1)} async-done(((bf16[8,5,2048]{2,1,0:T(8,128)(2,1)}), bf16[8,5,2048]{2,1,0:T(8,128)(2,1)S(1)}, u32[]{:S(2)}, u32[]{:S(2)}) %all-to-all-start) | async-done | bytes 163872 | tf_op jit(solution)/shard_map/while/body/eval_jaxpr/all_to_all | solution.py:54
  100.3 9.6 %all-to-all-done.1 = bf16[8,5,2048]{2,1,0:T(8,128)(2,1)S(1)} async-done(((bf16[8,5,2048]{2,1,0:T(8,128)(2,1)}), bf16[8,5,2048]{2,1,0:T(8,128)(2,1)S(1)}, u32[]{:S(2)}, u32[]{:S(2)}) %all-to-all-start.1) | async-done | bytes 163872 | tf_op jit(solution)/shard_map/while/body/eval_jaxpr/all_to_all | solution.py:56
  112.6 38.1 %collective-permute-done = bf16[3,8,2048]{2,1,0:T(8,128)(2,1)S(1)} collective-permute-done((bf16[3,8,2048]{2,1,0:T(8,128)(2,1)S(1)}, bf16[3,8,2048]{2,1,0:T(8,128)(2,1)S(1)}, u32[]{:S(2)}, u32[]{:S(2)}) %collective-permute-start) | collective-permute-done | bytes 98336 | tf_op jit(solution)/shard_map/while/body/eval_jaxpr/ppermute | solution.py:16
  157.4 9.6 %all-to-all-done = bf16[8,5,2048]{2,1,0:T(8,128)(2,1)S(1)} async-done(((bf16[8,5,2048]{2,1,0:T(8,128)(2,1)}), bf16[8,5,2048]{2,1,0:T(8,128)(2,1)S(1)}, u32[]{:S(2)}, u32[]{:S(2)}) %all-to-all-start) | async-done | bytes 163872 | tf_op jit(solution)/shard_map/while/body/eval_jaxpr/all_to_all | solution.py:54
  167.0 13.1 %conditional.2 = (bf16[8,5,2048]{2,1,0:T(8,128)(2,1)}) conditional(s32[]{:T(128)} %convert_element_type.138, () %tuple.73, (bf16[8,5,2048]{2,1,0:T(8,128)(2,1)S(1)}, bf16[2048,1792]{1,0:T(8,128)(2,1)}, bf16[2048,1792]{1,0:T(8,128)(2,1)}, bf16[1792,2048]{1,0:T(8,128)(2,1)}) %tuple.74), branch_computations={%region_4.4_spmd, %region_5.5_spmd} | conditional | flops 881315840 | bytes 23740424 | solution.py:55
  183.5 9.6 %all-to-all-done.1 = bf16[8,5,2048]{2,1,0:T(8,128)(2,1)S(1)} async-done(((bf16[8,5,2048]{2,1,0:T(8,128)(2,1)}), bf16[8,5,2048]{2,1,0:T(8,128)(2,1)S(1)}, u32[]{:S(2)}, u32[]{:S(2)}) %all-to-all-start.1) | async-done | bytes 163872 | tf_op jit(solution)/shard_map/while/body/eval_jaxpr/all_to_all | solution.py:56
  208.7 9.6 %all-to-all-done = bf16[8,5,2048]{2,1,0:T(8,128)(2,1)S(1)} async-done(((bf16[8,5,2048]{2,1,0:T(8,128)(2,1)}), bf16[8,5,2048]{2,1,0:T(8,128)(2,1)S(1)}, u32[]{:S(2)}, u32[]{:S(2)}) %all-to-all-start) | async-done | bytes 163872 | tf_op jit(solution)/shard_map/while/body/eval_jaxpr/all_to_all | solution.py:54
  218.3 13.1 %conditional.2 = (bf16[8,5,2048]{2,1,0:T(8,128)(2,1)}) conditional(s32[]{:T(128)} %convert_element_type.138, () %tuple.73, (bf16[8,5,2048]{2,1,0:T(8,128)(2,1)S(1)}, bf16[2048,1792]{1,0:T(8,128)(2,1)}, bf16[2048,1792]{1,0:T(8,128)(2,1)}, bf16[1792,2048]{1,0:T(8,128)(2,1)}) %tuple.74), branch_computations={%region_4.4_spmd, %region_5.5_spmd} | conditional | flops 881315840 | bytes 23740424 | solution.py:55
  234.8 9.6 %all-to-all-done.1 = bf16[8,5,2048]{2,1,0:T(8,128)(2,1)S(1)} async-done(((bf16[8,5,2048]{2,1,0:T(8,128)(2,1)}), bf16[8,5,2048]{2,1,0:T(8,128)(2,1)S(1)}, u32[]{:S(2)}, u32[]{:S(2)}) %all-to-all-start.1) | async-done | bytes 163872 | tf_op jit(solution)/shard_map/while/body/eval_jaxpr/all_to_all | solution.py:56
  259.9 9.6 %all-to-all-done = bf16[8,5,2048]{2,1,0:T(8,128)(2,1)S(1)} async-done(((bf16[8,5,2048]{2,1,0:T(8,128)(2,1)}), bf16[8,5,2048]{2,1,0:T(8,128)(2,1)S(1)}, u32[]{:S(2)}, u32[]{:S(2)}) %all-to-all-start) | async-done | bytes 163872 | tf_op jit(solution)/shard_map/while/body/eval_jaxpr/all_to_all | solution.py:54
  269.5 13.1 %conditional.2 = (bf16[8,5,2048]{2,1,0:T(8,128)(2,1)}) conditional(s32[]{:T(128)} %convert_element_type.138, () %tuple.73, (bf16[8,5,2048]{2,1,0:T(8,128)(2,1)S(1)}, bf16[2048,1792]{1,0:T(8,128)(2,1)}, bf16[2048,1792]{1,0:T(8,128)(2,1)}, bf16[1792,2048]{1,0:T(8,128)(2,1)}) %tuple.74), branch_computations={%region_4.4_spmd, %region_5.5_spmd} | conditional | flops 881315840 | bytes 23740424 | solution.py:55
  286.1 9.6 %all-to-all-done.1 = bf16[8,5,2048]{2,1,0:T(8,128)(2,1)S(1)} async-done(((bf16[8,5,2048]{2,1,0:T(8,128)(2,1)}), bf16[8,5,2048]{2,1,0:T(8,128)(2,1)S(1)}, u32[]{:S(2)}, u32[]{:S(2)}) %all-to-all-start.1) | async-done | bytes 163872 | tf_op jit(solution)/shard_map/while/body/eval_jaxpr/all_to_all | solution.py:56
  311.2 9.6 %all-to-all-done = bf16[8,5,2048]{2,1,0:T(8,128)(2,1)S(1)} async-done(((bf16[8,5,2048]{2,1,0:T(8,128)(2,1)}), bf16[8,5,2048]{2,1,0:T(8,128)(2,1)S(1)}, u32[]{:S(2)}, u32[]{:S(2)}) %all-to-all-start) | async-done | bytes 163872 | tf_op jit(solution)/shard_map/while/body/eval_jaxpr/all_to_all | solution.py:54
  320.8 13.1 %conditional.2 = (bf16[8,5,2048]{2,1,0:T(8,128)(2,1)}) conditional(s32[]{:T(128)} %convert_element_type.138, () %tuple.73, (bf16[8,5,2048]{2,1,0:T(8,128)(2,1)S(1)}, bf16[2048,1792]{1,0:T(8,128)(2,1)}, bf16[2048,1792]{1,0:T(8,128)(2,1)}, bf16[1792,2048]{1,0:T(8,128)(2,1)}) %tuple.74), branch_computations={%region_4.4_spmd, %region_5.5_spmd} | conditional | flops 881315840 | bytes 23740424 | solution.py:55
  337.3 9.6 %all-to-all-done.1 = bf16[8,5,2048]{2,1,0:T(8,128)(2,1)S(1)} async-done(((bf16[8,5,2048]{2,1,0:T(8,128)(2,1)}), bf16[8,5,2048]{2,1,0:T(8,128)(2,1)S(1)}, u32[]{:S(2)}, u32[]{:S(2)}) %all-to-all-start.1) | async-done | bytes 163872 | tf_op jit(solution)/shard_map/while/body/eval_jaxpr/all_to_all | solution.py:56
  362.5 9.6 %all-to-all-done = bf16[8,5,2048]{2,1,0:T(8,128)(2,1)S(1)} async-done(((bf16[8,5,2048]{2,1,0:T(8,128)(2,1)}), bf16[8,5,2048]{2,1,0:T(8,128)(2,1)S(1)}, u32[]{:S(2)}, u32[]{:S(2)}) %all-to-all-start) | async-done | bytes 163872 | tf_op jit(solution)/shard_map/while/body/eval_jaxpr/all_to_all | solution.py:54
  372.0 13.1 %conditional.2 = (bf16[8,5,2048]{2,1,0:T(8,128)(2,1)}) conditional(s32[]{:T(128)} %convert_element_type.138, () %tuple.73, (bf16[8,5,2048]{2,1,0:T(8,128)(2,1)S(1)}, bf16[2048,1792]{1,0:T(8,128)(2,1)}, bf16[2048,1792]{1,0:T(8,128)(2,1)}, bf16[1792,2048]{1,0:T(8,128)(2,1)}) %tuple.74), branch_computations={%region_4.4_spmd, %region_5.5_spmd} | conditional | flops 881315840 | bytes 23740424 | solution.py:55
  388.6 9.6 %all-to-all-done.1 = bf16[8,5,2048]{2,1,0:T(8,128)(2,1)S(1)} async-done(((bf16[8,5,2048]{2,1,0:T(8,128)(2,1)}), bf16[8,5,2048]{2,1,0:T(8,128)(2,1)S(1)}, u32[]{:S(2)}, u32[]{:S(2)}) %all-to-all-start.1) | async-done | bytes 163872 | tf_op jit(solution)/shard_map/while/body/eval_jaxpr/all_to_all | solution.py:56
  413.7 9.6 %all-to-all-done = bf16[8,5,2048]{2,1,0:T(8,128)(2,1)S(1)} async-done(((bf16[8,5,2048]{2,1,0:T(8,128)(2,1)}), bf16[8,5,2048]{2,1,0:T(8,128)(2,1)S(1)}, u32[]{:S(2)}, u32[]{:S(2)}) %all-to-all-start) | async-done | bytes 163872 | tf_op jit(solution)/shard_map/while/body/eval_jaxpr/all_to_all | solution.py:54
  423.3 13.1 %conditional.2 = (bf16[8,5,2048]{2,1,0:T(8,128)(2,1)}) conditional(s32[]{:T(128)} %convert_element_type.138, () %tuple.73, (bf16[8,5,2048]{2,1,0:T(8,128)(2,1)S(1)}, bf16[2048,1792]{1,0:T(8,128)(2,1)}, bf16[2048,1792]{1,0:T(8,128)(2,1)}, bf16[1792,2048]{1,0:T(8,128)(2,1)}) %tuple.74), branch_computations={%region_4.4_spmd, %region_5.5_spmd} | conditional | flops 881315840 | bytes 23740424 | solution.py:55
  439.8 9.6 %all-to-all-done.1 = bf16[8,5,2048]{2,1,0:T(8,128)(2,1)S(1)} async-done(((bf16[8,5,2048]{2,1,0:T(8,128)(2,1)}), bf16[8,5,2048]{2,1,0:T(8,128)(2,1)S(1)}, u32[]{:S(2)}, u32[]{:S(2)}) %all-to-all-start.1) | async-done | bytes 163872 | tf_op jit(solution)/shard_map/while/body/eval_jaxpr/all_to_all | solution.py:56
  465.0 9.6 %all-to-all-done = bf16[8,5,2048]{2,1,0:T(8,128)(2,1)S(1)} async-done(((bf16[8,5,2048]{2,1,0:T(8,128)(2,1)}), bf16[8,5,2048]{2,1,0:T(8,128)(2,1)S(1)}, u32[]{:S(2)}, u32[]{:S(2)}) %all-to-all-start) | async-done | bytes 163872 | tf_op jit(solution)/shard_map/while/body/eval_jaxpr/all_to_all | solution.py:54
  474.5 13.1 %conditional.2 = (bf16[8,5,2048]{2,1,0:T(8,128)(2,1)}) conditional(s32[]{:T(128)} %convert_element_type.138, () %tuple.73, (bf16[8,5,2048]{2,1,0:T(8,128)(2,1)S(1)}, bf16[2048,1792]{1,0:T(8,128)(2,1)}, bf16[2048,1792]{1,0:T(8,128)(2,1)}, bf16[1792,2048]{1,0:T(8,128)(2,1)}) %tuple.74), branch_computations={%region_4.4_spmd, %region_5.5_spmd} | conditional | flops 881315840 | bytes 23740424 | solution.py:55
  491.1 9.6 %all-to-all-done.1 = bf16[8,5,2048]{2,1,0:T(8,128)(2,1)S(1)} async-done(((bf16[8,5,2048]{2,1,0:T(8,128)(2,1)}), bf16[8,5,2048]{2,1,0:T(8,128)(2,1)S(1)}, u32[]{:S(2)}, u32[]{:S(2)}) %all-to-all-start.1) | async-done | bytes 163872 | tf_op jit(solution)/shard_map/while/body/eval_jaxpr/all_to_all | solution.py:56
  516.2 9.6 %all-to-all-done = bf16[8,5,2048]{2,1,0:T(8,128)(2,1)S(1)} async-done(((bf16[8,5,2048]{2,1,0:T(8,128)(2,1)}), bf16[8,5,2048]{2,1,0:T(8,128)(2,1)S(1)}, u32[]{:S(2)}, u32[]{:S(2)}) %all-to-all-start) | async-done | bytes 163872 | tf_op jit(solution)/shard_map/while/body/eval_jaxpr/all_to_all | solution.py:54
  525.8 13.1 %conditional.2 = (bf16[8,5,2048]{2,1,0:T(8,128)(2,1)}) conditional(s32[]{:T(128)} %convert_element_type.138, () %tuple.73, (bf16[8,5,2048]{2,1,0:T(8,128)(2,1)S(1)}, bf16[2048,1792]{1,0:T(8,128)(2,1)}, bf16[2048,1792]{1,0:T(8,128)(2,1)}, bf16[1792,2048]{1,0:T(8,128)(2,1)}) %tuple.74), branch_computations={%region_4.4_spmd, %region_5.5_spmd} | conditional | flops 881315840 | bytes 23740424 | solution.py:55
  542.3 9.6 %all-to-all-done.1 = bf16[8,5,2048]{2,1,0:T(8,128)(2,1)S(1)} async-done(((bf16[8,5,2048]{2,1,0:T(8,128)(2,1)}), bf16[8,5,2048]{2,1,0:T(8,128)(2,1)S(1)}, u32[]{:S(2)}, u32[]{:S(2)}) %all-to-all-start.1) | async-done | bytes 163872 | tf_op jit(solution)/shard_map/while/body/eval_jaxpr/all_to_all | solution.py:56
  (337 shorter events, 311.6 us)
Async XLA Ops:
  5.5 14.6 %all-to-all-start = ((bf16[8,5,2048]{2,1,0:T(8,128)(2,1)}), bf16[8,5,2048]{2,1,0:T(8,128)(2,1)S(1)}, u32[]{:S(2)}, u32[]{:S(2)}) async-start(bf16[8,5,2048]{2,1,0:T(8,128)(2,1)} %bitcast.98), calls=%async_computation | async-start | bytes 524288 | tf_op jit(solution)/shard_map/while/body/eval_jaxpr/all_to_all | solution.py:54
  20.8 13.1 %all-to-all-start.1 = ((bf16[8,5,2048]{2,1,0:T(8,128)(2,1)}), bf16[8,5,2048]{2,1,0:T(8,128)(2,1)S(1)}, u32[]{:S(2)}, u32[]{:S(2)}) async-start(bf16[8,5,2048]{2,1,0:T(8,128)(2,1)} %get-tuple-element.654), calls=%async_computation.1 | async-start | bytes 524288 | tf_op jit(solution)/shard_map/while/body/eval_jaxpr/all_to_all | solution.py:56
  35.3 6.5 %collective-permute-start = (bf16[3,8,2048]{2,1,0:T(8,128)(2,1)S(1)}, bf16[3,8,2048]{2,1,0:T(8,128)(2,1)S(1)}, u32[]{:S(2)}, u32[]{:S(2)}) collective-permute-start(bf16[3,8,2048]{2,1,0:T(8,128)(2,1)S(1)} %maximum_select_fusion.2), channel_id=1, source_target_pairs={{0,8},{8,16},{16,24},{1,9},{9,17},{17,25},{2,10},{10,18},{18,26},{... | collective-permute-start | bytes 294920 | tf_op jit(solution)/shard_map/while/body/eval_jaxpr/ppermute | solution.py:16
  45.0 13.1 %all-to-all-start = ((bf16[8,5,2048]{2,1,0:T(8,128)(2,1)}), bf16[8,5,2048]{2,1,0:T(8,128)(2,1)S(1)}, u32[]{:S(2)}, u32[]{:S(2)}) async-start(bf16[8,5,2048]{2,1,0:T(8,128)(2,1)} %bitcast.98), calls=%async_computation | async-start | bytes 524288 | tf_op jit(solution)/shard_map/while/body/eval_jaxpr/all_to_all | solution.py:54
  58.8 13.1 %all-to-all-start.1 = ((bf16[8,5,2048]{2,1,0:T(8,128)(2,1)}), bf16[8,5,2048]{2,1,0:T(8,128)(2,1)S(1)}, u32[]{:S(2)}, u32[]{:S(2)}) async-start(bf16[8,5,2048]{2,1,0:T(8,128)(2,1)} %get-tuple-element.654), calls=%async_computation.1 | async-start | bytes 524288 | tf_op jit(solution)/shard_map/while/body/eval_jaxpr/all_to_all | solution.py:56
  83.0 13.1 %all-to-all-start = ((bf16[8,5,2048]{2,1,0:T(8,128)(2,1)}), bf16[8,5,2048]{2,1,0:T(8,128)(2,1)S(1)}, u32[]{:S(2)}, u32[]{:S(2)}) async-start(bf16[8,5,2048]{2,1,0:T(8,128)(2,1)} %bitcast.98), calls=%async_computation | async-start | bytes 524288 | tf_op jit(solution)/shard_map/while/body/eval_jaxpr/all_to_all | solution.py:54
  96.8 13.1 %all-to-all-start.1 = ((bf16[8,5,2048]{2,1,0:T(8,128)(2,1)}), bf16[8,5,2048]{2,1,0:T(8,128)(2,1)S(1)}, u32[]{:S(2)}, u32[]{:S(2)}) async-start(bf16[8,5,2048]{2,1,0:T(8,128)(2,1)} %get-tuple-element.654), calls=%async_computation.1 | async-start | bytes 524288 | tf_op jit(solution)/shard_map/while/body/eval_jaxpr/all_to_all | solution.py:56
  111.3 39.4 %collective-permute-start = (bf16[3,8,2048]{2,1,0:T(8,128)(2,1)S(1)}, bf16[3,8,2048]{2,1,0:T(8,128)(2,1)S(1)}, u32[]{:S(2)}, u32[]{:S(2)}) collective-permute-start(bf16[3,8,2048]{2,1,0:T(8,128)(2,1)S(1)} %maximum_select_fusion.2), channel_id=1, source_target_pairs={{0,8},{8,16},{16,24},{1,9},{9,17},{17,25},{2,10},{10,18},{18,26},{... | collective-permute-start | bytes 294920 | tf_op jit(solution)/shard_map/while/body/eval_jaxpr/ppermute | solution.py:16
  154.0 13.1 %all-to-all-start = ((bf16[8,5,2048]{2,1,0:T(8,128)(2,1)}), bf16[8,5,2048]{2,1,0:T(8,128)(2,1)S(1)}, u32[]{:S(2)}, u32[]{:S(2)}) async-start(bf16[8,5,2048]{2,1,0:T(8,128)(2,1)} %bitcast.98), calls=%async_computation | async-start | bytes 524288 | tf_op jit(solution)/shard_map/while/body/eval_jaxpr/all_to_all | solution.py:54
  180.1 13.1 %all-to-all-start.1 = ((bf16[8,5,2048]{2,1,0:T(8,128)(2,1)}), bf16[8,5,2048]{2,1,0:T(8,128)(2,1)S(1)}, u32[]{:S(2)}, u32[]{:S(2)}) async-start(bf16[8,5,2048]{2,1,0:T(8,128)(2,1)} %get-tuple-element.654), calls=%async_computation.1 | async-start | bytes 524288 | tf_op jit(solution)/shard_map/while/body/eval_jaxpr/all_to_all | solution.py:56
  194.5 7.4 %collective-permute-start = (bf16[3,8,2048]{2,1,0:T(8,128)(2,1)S(1)}, bf16[3,8,2048]{2,1,0:T(8,128)(2,1)S(1)}, u32[]{:S(2)}, u32[]{:S(2)}) collective-permute-start(bf16[3,8,2048]{2,1,0:T(8,128)(2,1)S(1)} %maximum_select_fusion.2), channel_id=1, source_target_pairs={{0,8},{8,16},{16,24},{1,9},{9,17},{17,25},{2,10},{10,18},{18,26},{... | collective-permute-start | bytes 294920 | tf_op jit(solution)/shard_map/while/body/eval_jaxpr/ppermute | solution.py:16
  205.2 13.1 %all-to-all-start = ((bf16[8,5,2048]{2,1,0:T(8,128)(2,1)}), bf16[8,5,2048]{2,1,0:T(8,128)(2,1)S(1)}, u32[]{:S(2)}, u32[]{:S(2)}) async-start(bf16[8,5,2048]{2,1,0:T(8,128)(2,1)} %bitcast.98), calls=%async_computation | async-start | bytes 524288 | tf_op jit(solution)/shard_map/while/body/eval_jaxpr/all_to_all | solution.py:54
  231.3 13.1 %all-to-all-start.1 = ((bf16[8,5,2048]{2,1,0:T(8,128)(2,1)}), bf16[8,5,2048]{2,1,0:T(8,128)(2,1)S(1)}, u32[]{:S(2)}, u32[]{:S(2)}) async-start(bf16[8,5,2048]{2,1,0:T(8,128)(2,1)} %get-tuple-element.654), calls=%async_computation.1 | async-start | bytes 524288 | tf_op jit(solution)/shard_map/while/body/eval_jaxpr/all_to_all | solution.py:56
  245.8 7.4 %collective-permute-start = (bf16[3,8,2048]{2,1,0:T(8,128)(2,1)S(1)}, bf16[3,8,2048]{2,1,0:T(8,128)(2,1)S(1)}, u32[]{:S(2)}, u32[]{:S(2)}) collective-permute-start(bf16[3,8,2048]{2,1,0:T(8,128)(2,1)S(1)} %maximum_select_fusion.2), channel_id=1, source_target_pairs={{0,8},{8,16},{16,24},{1,9},{9,17},{17,25},{2,10},{10,18},{18,26},{... | collective-permute-start | bytes 294920 | tf_op jit(solution)/shard_map/while/body/eval_jaxpr/ppermute | solution.py:16
  256.5 13.1 %all-to-all-start = ((bf16[8,5,2048]{2,1,0:T(8,128)(2,1)}), bf16[8,5,2048]{2,1,0:T(8,128)(2,1)S(1)}, u32[]{:S(2)}, u32[]{:S(2)}) async-start(bf16[8,5,2048]{2,1,0:T(8,128)(2,1)} %bitcast.98), calls=%async_computation | async-start | bytes 524288 | tf_op jit(solution)/shard_map/while/body/eval_jaxpr/all_to_all | solution.py:54
  282.6 13.1 %all-to-all-start.1 = ((bf16[8,5,2048]{2,1,0:T(8,128)(2,1)}), bf16[8,5,2048]{2,1,0:T(8,128)(2,1)S(1)}, u32[]{:S(2)}, u32[]{:S(2)}) async-start(bf16[8,5,2048]{2,1,0:T(8,128)(2,1)} %get-tuple-element.654), calls=%async_computation.1 | async-start | bytes 524288 | tf_op jit(solution)/shard_map/while/body/eval_jaxpr/all_to_all | solution.py:56
  297.0 7.4 %collective-permute-start = (bf16[3,8,2048]{2,1,0:T(8,128)(2,1)S(1)}, bf16[3,8,2048]{2,1,0:T(8,128)(2,1)S(1)}, u32[]{:S(2)}, u32[]{:S(2)}) collective-permute-start(bf16[3,8,2048]{2,1,0:T(8,128)(2,1)S(1)} %maximum_select_fusion.2), channel_id=1, source_target_pairs={{0,8},{8,16},{16,24},{1,9},{9,17},{17,25},{2,10},{10,18},{18,26},{... | collective-permute-start | bytes 294920 | tf_op jit(solution)/shard_map/while/body/eval_jaxpr/ppermute | solution.py:16
  307.7 13.1 %all-to-all-start = ((bf16[8,5,2048]{2,1,0:T(8,128)(2,1)}), bf16[8,5,2048]{2,1,0:T(8,128)(2,1)S(1)}, u32[]{:S(2)}, u32[]{:S(2)}) async-start(bf16[8,5,2048]{2,1,0:T(8,128)(2,1)} %bitcast.98), calls=%async_computation | async-start | bytes 524288 | tf_op jit(solution)/shard_map/while/body/eval_jaxpr/all_to_all | solution.py:54
  333.9 13.1 %all-to-all-start.1 = ((bf16[8,5,2048]{2,1,0:T(8,128)(2,1)}), bf16[8,5,2048]{2,1,0:T(8,128)(2,1)S(1)}, u32[]{:S(2)}, u32[]{:S(2)}) async-start(bf16[8,5,2048]{2,1,0:T(8,128)(2,1)} %get-tuple-element.654), calls=%async_computation.1 | async-start | bytes 524288 | tf_op jit(solution)/shard_map/while/body/eval_jaxpr/all_to_all | solution.py:56
  348.3 7.4 %collective-permute-start = (bf16[3,8,2048]{2,1,0:T(8,128)(2,1)S(1)}, bf16[3,8,2048]{2,1,0:T(8,128)(2,1)S(1)}, u32[]{:S(2)}, u32[]{:S(2)}) collective-permute-start(bf16[3,8,2048]{2,1,0:T(8,128)(2,1)S(1)} %maximum_select_fusion.2), channel_id=1, source_target_pairs={{0,8},{8,16},{16,24},{1,9},{9,17},{17,25},{2,10},{10,18},{18,26},{... | collective-permute-start | bytes 294920 | tf_op jit(solution)/shard_map/while/body/eval_jaxpr/ppermute | solution.py:16
  359.0 13.1 %all-to-all-start = ((bf16[8,5,2048]{2,1,0:T(8,128)(2,1)}), bf16[8,5,2048]{2,1,0:T(8,128)(2,1)S(1)}, u32[]{:S(2)}, u32[]{:S(2)}) async-start(bf16[8,5,2048]{2,1,0:T(8,128)(2,1)} %bitcast.98), calls=%async_computation | async-start | bytes 524288 | tf_op jit(solution)/shard_map/while/body/eval_jaxpr/all_to_all | solution.py:54
  385.1 13.1 %all-to-all-start.1 = ((bf16[8,5,2048]{2,1,0:T(8,128)(2,1)}), bf16[8,5,2048]{2,1,0:T(8,128)(2,1)S(1)}, u32[]{:S(2)}, u32[]{:S(2)}) async-start(bf16[8,5,2048]{2,1,0:T(8,128)(2,1)} %get-tuple-element.654), calls=%async_computation.1 | async-start | bytes 524288 | tf_op jit(solution)/shard_map/while/body/eval_jaxpr/all_to_all | solution.py:56
  399.6 7.4 %collective-permute-start = (bf16[3,8,2048]{2,1,0:T(8,128)(2,1)S(1)}, bf16[3,8,2048]{2,1,0:T(8,128)(2,1)S(1)}, u32[]{:S(2)}, u32[]{:S(2)}) collective-permute-start(bf16[3,8,2048]{2,1,0:T(8,128)(2,1)S(1)} %maximum_select_fusion.2), channel_id=1, source_target_pairs={{0,8},{8,16},{16,24},{1,9},{9,17},{17,25},{2,10},{10,18},{18,26},{... | collective-permute-start | bytes 294920 | tf_op jit(solution)/shard_map/while/body/eval_jaxpr/ppermute | solution.py:16
  410.2 13.1 %all-to-all-start = ((bf16[8,5,2048]{2,1,0:T(8,128)(2,1)}), bf16[8,5,2048]{2,1,0:T(8,128)(2,1)S(1)}, u32[]{:S(2)}, u32[]{:S(2)}) async-start(bf16[8,5,2048]{2,1,0:T(8,128)(2,1)} %bitcast.98), calls=%async_computation | async-start | bytes 524288 | tf_op jit(solution)/shard_map/while/body/eval_jaxpr/all_to_all | solution.py:54
  436.4 13.1 %all-to-all-start.1 = ((bf16[8,5,2048]{2,1,0:T(8,128)(2,1)}), bf16[8,5,2048]{2,1,0:T(8,128)(2,1)S(1)}, u32[]{:S(2)}, u32[]{:S(2)}) async-start(bf16[8,5,2048]{2,1,0:T(8,128)(2,1)} %get-tuple-element.654), calls=%async_computation.1 | async-start | bytes 524288 | tf_op jit(solution)/shard_map/while/body/eval_jaxpr/all_to_all | solution.py:56
  450.8 7.4 %collective-permute-start = (bf16[3,8,2048]{2,1,0:T(8,128)(2,1)S(1)}, bf16[3,8,2048]{2,1,0:T(8,128)(2,1)S(1)}, u32[]{:S(2)}, u32[]{:S(2)}) collective-permute-start(bf16[3,8,2048]{2,1,0:T(8,128)(2,1)S(1)} %maximum_select_fusion.2), channel_id=1, source_target_pairs={{0,8},{8,16},{16,24},{1,9},{9,17},{17,25},{2,10},{10,18},{18,26},{... | collective-permute-start | bytes 294920 | tf_op jit(solution)/shard_map/while/body/eval_jaxpr/ppermute | solution.py:16
  461.5 13.1 %all-to-all-start = ((bf16[8,5,2048]{2,1,0:T(8,128)(2,1)}), bf16[8,5,2048]{2,1,0:T(8,128)(2,1)S(1)}, u32[]{:S(2)}, u32[]{:S(2)}) async-start(bf16[8,5,2048]{2,1,0:T(8,128)(2,1)} %bitcast.98), calls=%async_computation | async-start | bytes 524288 | tf_op jit(solution)/shard_map/while/body/eval_jaxpr/all_to_all | solution.py:54
  487.6 13.1 %all-to-all-start.1 = ((bf16[8,5,2048]{2,1,0:T(8,128)(2,1)}), bf16[8,5,2048]{2,1,0:T(8,128)(2,1)S(1)}, u32[]{:S(2)}, u32[]{:S(2)}) async-start(bf16[8,5,2048]{2,1,0:T(8,128)(2,1)} %get-tuple-element.654), calls=%async_computation.1 | async-start | bytes 524288 | tf_op jit(solution)/shard_map/while/body/eval_jaxpr/all_to_all | solution.py:56
  502.1 7.4 %collective-permute-start = (bf16[3,8,2048]{2,1,0:T(8,128)(2,1)S(1)}, bf16[3,8,2048]{2,1,0:T(8,128)(2,1)S(1)}, u32[]{:S(2)}, u32[]{:S(2)}) collective-permute-start(bf16[3,8,2048]{2,1,0:T(8,128)(2,1)S(1)} %maximum_select_fusion.2), channel_id=1, source_target_pairs={{0,8},{8,16},{16,24},{1,9},{9,17},{17,25},{2,10},{10,18},{18,26},{... | collective-permute-start | bytes 294920 | tf_op jit(solution)/shard_map/while/body/eval_jaxpr/ppermute | solution.py:16
  512.7 13.1 %all-to-all-start = ((bf16[8,5,2048]{2,1,0:T(8,128)(2,1)}), bf16[8,5,2048]{2,1,0:T(8,128)(2,1)S(1)}, u32[]{:S(2)}, u32[]{:S(2)}) async-start(bf16[8,5,2048]{2,1,0:T(8,128)(2,1)} %bitcast.98), calls=%async_computation | async-start | bytes 524288 | tf_op jit(solution)/shard_map/while/body/eval_jaxpr/all_to_all | solution.py:54
  538.9 13.1 %all-to-all-start.1 = ((bf16[8,5,2048]{2,1,0:T(8,128)(2,1)}), bf16[8,5,2048]{2,1,0:T(8,128)(2,1)S(1)}, u32[]{:S(2)}, u32[]{:S(2)}) async-start(bf16[8,5,2048]{2,1,0:T(8,128)(2,1)} %get-tuple-element.654), calls=%async_computation.1 | async-start | bytes 524288 | tf_op jit(solution)/shard_map/while/body/eval_jaxpr/all_to_all | solution.py:56
  553.3 6.5 %collective-permute-start = (bf16[3,8,2048]{2,1,0:T(8,128)(2,1)S(1)}, bf16[3,8,2048]{2,1,0:T(8,128)(2,1)S(1)}, u32[]{:S(2)}, u32[]{:S(2)}) collective-permute-start(bf16[3,8,2048]{2,1,0:T(8,128)(2,1)S(1)} %maximum_select_fusion.2), channel_id=1, source_target_pairs={{0,8},{8,16},{16,24},{1,9},{9,17},{17,25},{2,10},{10,18},{18,26},{... | collective-permute-start | bytes 294920 | tf_op jit(solution)/shard_map/while/body/eval_jaxpr/ppermute | solution.py:16
  (3 other events, 9.4 us)
where the time goes:
time: 564 us; the launch traced here: 561 us
  waiting for transfers between devices  307 us (54%)
  matrix products  97.6 us (17%)
  starting transfers between devices  90.8 us (16%)
  local copies, waits for them, and re-layouts  33.4 us (6%)
  other arithmetic  29.3 us (5%)
    all_to_all x11, waiting for transfers between devices, run_experts(): lax.all_to_all(computed, 'expert', split_axis=0, concat_axis=0, tiled=True)  106 us
    all_to_all x11, waiting for transfers between devices, run_experts(): lax.all_to_all(outgoing, 'expert', split_axis=0, concat_axis=0, tiled=True)  105 us
    ppermute x11, waiting for transfers between devices, shifted(): return lax.ppermute(value, axis, pairs)  96.5 us
    dot_general x8, matrix products, expert_rows(): jnp.dot(hidden, down_mat, preferred_element_type=jnp.float32)  62.1 us
    all_to_all x11, starting transfers between devices, run_experts(): lax.all_to_all(outgoing, 'expert', split_axis=0, concat_axis=0, tiled=True)  39 us
    all_to_all x11, starting transfers between devices, run_experts(): lax.all_to_all(computed, 'expert', split_axis=0, concat_axis=0, tiled=True)  37.5 us
    dot_general x8, matrix products, expert_rows(): gate_vals = jnp.dot(flat_rows, gate_mat, preferred_element_type=jnp.float32)  35.5 us
    ppermute x11, starting transfers between devices, shifted(): return lax.ppermute(value, axis, pairs)  14.2 us
  transfers between devices with their start and end apart: 33, of which 33 were waited for; matrix products, arithmetic and copies ran while one was open for 0% of the time, Pallas kernels for 0%

commit v1 on v0

--- a/solution.py
+++ b/solution.py
@@ -51,7 +51,19 @@
         return jnp.zeros(received.shape, jnp.bfloat16)
 
     def run_experts(outgoing, active):
-        received = lax.all_to_all(outgoing, "expert", split_axis=0, concat_axis=0, tiled=True)
+        ways, here = (lax.axis_size("expert"), lax.axis_index("expert"))
+        width = outgoing.shape[0] // ways
+        shape = list(outgoing.shape)
+        shape[0] = width
+        height = shape[0]
+        shape[0] = height * ways
+        full = jnp.zeros(shape, outgoing.dtype)
+        for mask in range(ways):
+            part = lax.dynamic_slice_in_dim(outgoing, (here ^ mask) * width, width, axis=0)
+            if mask:
+                part = lax.ppermute(part, "expert", [(d, d ^ mask) for d in range(ways)])
+            full = lax.dynamic_update_slice_in_dim(full, part, (here ^ mask) * height, axis=0)
+        received = full
         computed = lax.cond(active, expert_rows, skip_rows, received)
         returned = lax.all_to_all(computed, "expert", split_axis=0, concat_axis=0, tiled=True)
         return returned

time: 564 us -> 542 us (0.961)
  waiting for transfers between devices: 307 us -> 240 us
  starting transfers between devices: 90.8 us -> 142 us
  local copies, waits for them, and re-layouts: 33.4 us -> 26.8 us
    all_to_all x11 -> x0, waiting for transfers between devices: 105 us -> none  [run_experts(): lax.all_to_all(outgoing, 'expert', split_axis=0, concat_axis=0, tiled=True)]
    ppermute x0 -> x77, starting transfers between devices: none -> 90 us  [run_experts(): part = lax.ppermute(part, 'expert', [(d, d ^ mask) for d in range(ways)])]
    all_to_all x11 -> x0, starting transfers between devices: 39 us -> none  [run_experts(): lax.all_to_all(outgoing, 'expert', split_axis=0, concat_axis=0, tiled=True)]
    ppermute x0 -> x77, waiting for transfers between devices: none -> 37.1 us  [run_experts(): part = lax.ppermute(part, 'expert', [(d, d ^ mask) for d in range(ways)])]
    broadcast_in_dim x11, local copies, waits for them, and re-layouts: 7.93 us -> 0.21 us  [advance(): outgoing = jnp.repeat(buffer, shards, axis=0)]
  transfers between devices with their start and end apart: 33 -> 99, of which waited for: 33 -> 45; matrix products, arithmetic and copies ran while one was open for 0% -> 0% of each run, Pallas kernels for 0% -> 0%
where the time goes in v1:
time: 542 us; the launch traced here: 539 us
  waiting for transfers between devices  240 us (44%)
  starting transfers between devices  142 us (26%)
  matrix products  97.6 us (18%)
  other arithmetic  29.2 us (5%)
  local copies, waits for them, and re-layouts  26.8 us (5%)
    all_to_all x11, waiting for transfers between devices, run_experts(): lax.all_to_all(computed, 'expert', split_axis=0, concat_axis=0, tiled=True)  106 us
    ppermute x11, waiting for transfers between devices, shifted(): return lax.ppermute(value, axis, pairs)  97 us
    ppermute x77, starting transfers between devices, run_experts(): part = lax.ppermute(part, 'expert', [(d, d ^ mask) for d in range(ways)])  90 us
    dot_general x8, matrix products, expert_rows(): jnp.dot(hidden, down_mat, preferred_element_type=jnp.float32)  62.1 us
    all_to_all x11, starting transfers between devices, run_experts(): lax.all_to_all(computed, 'expert', split_axis=0, concat_axis=0, tiled=True)  38.1 us
    ppermute x77, waiting for transfers between devices, run_experts(): part = lax.ppermute(part, 'expert', [(d, d ^ mask) for d in range(ways)])  37.1 us
    dot_general x8, matrix products, expert_rows(): gate_vals = jnp.dot(flat_rows, gate_mat, preferred_element_type=jnp.float32)  35.5 us
    ppermute x11, starting transfers between devices, shifted(): return lax.ppermute(value, axis, pairs)  14.2 us
  transfers between devices with their start and end apart: 99, of which 45 were waited for; matrix products, arithmetic and copies ran while one was open for 0% of the time, Pallas kernels for 0%

profile of v1, /device:TPU:6, one launch (start us, length us, event | category | flops | bytes accessed | tf_op | source)
XLA Modules:
  0.0 539.5 jit_solution(4210887245931107998)
XLA Ops:
  2.2 536.6 %while.17 = (s32[]{:T(128)}, bf16[3,8,2048]{2,1,0:T(8,128)(2,1)S(1)}, bf16[8,8,2048]{2,1,0:T(8,128)(2,1)S(1)}, pred[]{:T(512)}, pred[]{:T(512)}, /*index=5*/s32[...) while((s32[]{:T(128)}, ...), condition=%wide.region_7.8_spmd, body=%wide.region_0.7_spmd.sunk | while | flops 881903936 | bytes 27907788 | solution.py:121
  22.5 9.6 %all-to-all-done = bf16[8,5,2048]{2,1,0:T(8,128)(2,1)S(1)} async-done(((bf16[8,5,2048]{2,1,0:T(8,128)(2,1)}), bf16[8,5,2048]{2,1,0:T(8,128)(2,1)S(1)}, u32[]{:S(2)}, u32[]{:S(2)}) %all-to-all-start) | async-done | bytes 163872 | tf_op jit(solution)/shard_map/while/body/eval_jaxpr/all_to_all | solution.py:68
  58.3 9.7 %all-to-all-done = bf16[8,5,2048]{2,1,0:T(8,128)(2,1)S(1)} async-done(((bf16[8,5,2048]{2,1,0:T(8,128)(2,1)}), bf16[8,5,2048]{2,1,0:T(8,128)(2,1)S(1)}, u32[]{:S(2)}, u32[]{:S(2)}) %all-to-all-start) | async-done | bytes 163872 | tf_op jit(solution)/shard_map/while/body/eval_jaxpr/all_to_all | solution.py:68
  94.2 9.7 %all-to-all-done = bf16[8,5,2048]{2,1,0:T(8,128)(2,1)S(1)} async-done(((bf16[8,5,2048]{2,1,0:T(8,128)(2,1)}), bf16[8,5,2048]{2,1,0:T(8,128)(2,1)S(1)}, u32[]{:S(2)}, u32[]{:S(2)}) %all-to-all-start) | async-done | bytes 163872 | tf_op jit(solution)/shard_map/while/body/eval_jaxpr/all_to_all | solution.py:68
  106.6 38.6 %collective-permute-done.7 = bf16[3,8,2048]{2,1,0:T(8,128)(2,1)S(1)} collective-permute-done((bf16[3,8,2048]{2,1,0:T(8,128)(2,1)S(1)}, bf16[3,8,2048]{2,1,0:T(8,128)(2,1)S(1)}, u32[]{:S(2)}, u32[]{:S(2)}) %collective-permute-start.7) | collective-permute-done | bytes 98336 | tf_op jit(solution)/shard_map/while/body/eval_jaxpr/ppermute | solution.py:16
  159.4 13.3 %conditional.2 = (bf16[8,5,2048]{2,1,0:T(8,128)(2,1)}) conditional(s32[]{:T(128)} %convert_element_type.142, () %tuple.86, (s32[]{:T(128)}, bf16[8,5,2048]{2,1,0:T(8,128)(2,1)S(1)}, bf16[1,5,2048]{2,1,0:T(8,128)(2,1)S(1)}, s32[]{:T(128)}, bf16[1,5,2048]{2,1,0:T(8,128)(2,1)S(1)}, /*index=5*/s32[]{:T(128)}, bf16[1,5,2048]{2,1,0:T(8,128)(2,1)S(1)}, ...), branch_computations={%region_4.4_spmd, %region_5.5_spmd} | conditional | flops 881315840 | bytes 24428620 | solution.py:67
  164.1 7.8 %convolution_convert_fusion = bf16[40,2048]{1,0:T(8,128)(2,1)S(1)} fusion(bf16[1792,2048]{1,0:T(8,128)(2,1)} %get-tuple-element.515, bf16[40,2048]{1,0:T(8,128)(2,1)S(1)} %reshape.154, bf16[2048,1792]{1,0:T(8,128)(2,1)} %get-tuple-element.514, f32[40,1792]{1,0:T(8,128)S(1)} %fusion.25), kind=kOutput, calls=%fused_computation.6 | convolution fusion | flops 587714560 | bytes 15294464 | tf_op jit(solution)/shard_map/while/body/eval_jaxpr/cond/branch_1_fun/dot_general | solution.py:45
  176.1 9.6 %all-to-all-done = bf16[8,5,2048]{2,1,0:T(8,128)(2,1)S(1)} async-done(((bf16[8,5,2048]{2,1,0:T(8,128)(2,1)}), bf16[8,5,2048]{2,1,0:T(8,128)(2,1)S(1)}, u32[]{:S(2)}, u32[]{:S(2)}) %all-to-all-start) | async-done | bytes 163872 | tf_op jit(solution)/shard_map/while/body/eval_jaxpr/all_to_all | solution.py:68
  188.4 6.1 %collective-permute-done.7 = bf16[3,8,2048]{2,1,0:T(8,128)(2,1)S(1)} collective-permute-done((bf16[3,8,2048]{2,1,0:T(8,128)(2,1)S(1)}, bf16[3,8,2048]{2,1,0:T(8,128)(2,1)S(1)}, u32[]{:S(2)}, u32[]{:S(2)}) %collective-permute-start.7) | collective-permute-done | bytes 98336 | tf_op jit(solution)/shard_map/while/body/eval_jaxpr/ppermute | solution.py:16
  208.7 13.3 %conditional.2 = (bf16[8,5,2048]{2,1,0:T(8,128)(2,1)}) conditional(s32[]{:T(128)} %convert_element_type.142, () %tuple.86, (s32[]{:T(128)}, bf16[8,5,2048]{2,1,0:T(8,128)(2,1)S(1)}, bf16[1,5,2048]{2,1,0:T(8,128)(2,1)S(1)}, s32[]{:T(128)}, bf16[1,5,2048]{2,1,0:T(8,128)(2,1)S(1)}, /*index=5*/s32[]{:T(128)}, bf16[1,5,2048]{2,1,0:T(8,128)(2,1)S(1)}, ...), branch_computations={%region_4.4_spmd, %region_5.5_spmd} | conditional | flops 881315840 | bytes 24428620 | solution.py:67
  213.4 7.8 %convolution_convert_fusion = bf16[40,2048]{1,0:T(8,128)(2,1)S(1)} fusion(bf16[1792,2048]{1,0:T(8,128)(2,1)} %get-tuple-element.515, bf16[40,2048]{1,0:T(8,128)(2,1)S(1)} %reshape.154, bf16[2048,1792]{1,0:T(8,128)(2,1)} %get-tuple-element.514, f32[40,1792]{1,0:T(8,128)S(1)} %fusion.25), kind=kOutput, calls=%fused_computation.6 | convolution fusion | flops 587714560 | bytes 15294464 | tf_op jit(solution)/shard_map/while/body/eval_jaxpr/cond/branch_1_fun/dot_general | solution.py:45
  225.4 9.6 %all-to-all-done = bf16[8,5,2048]{2,1,0:T(8,128)(2,1)S(1)} async-done(((bf16[8,5,2048]{2,1,0:T(8,128)(2,1)}), bf16[8,5,2048]{2,1,0:T(8,128)(2,1)S(1)}, u32[]{:S(2)}, u32[]{:S(2)}) %all-to-all-start) | async-done | bytes 163872 | tf_op jit(solution)/shard_map/while/body/eval_jaxpr/all_to_all | solution.py:68
  258.0 13.3 %conditional.2 = (bf16[8,5,2048]{2,1,0:T(8,128)(2,1)}) conditional(s32[]{:T(128)} %convert_element_type.142, () %tuple.86, (s32[]{:T(128)}, bf16[8,5,2048]{2,1,0:T(8,128)(2,1)S(1)}, bf16[1,5,2048]{2,1,0:T(8,128)(2,1)S(1)}, s32[]{:T(128)}, bf16[1,5,2048]{2,1,0:T(8,128)(2,1)S(1)}, /*index=5*/s32[]{:T(128)}, bf16[1,5,2048]{2,1,0:T(8,128)(2,1)S(1)}, ...), branch_computations={%region_4.4_spmd, %region_5.5_spmd} | conditional | flops 881315840 | bytes 24428620 | solution.py:67
  262.7 7.8 %convolution_convert_fusion = bf16[40,2048]{1,0:T(8,128)(2,1)S(1)} fusion(bf16[1792,2048]{1,0:T(8,128)(2,1)} %get-tuple-element.515, bf16[40,2048]{1,0:T(8,128)(2,1)S(1)} %reshape.154, bf16[2048,1792]{1,0:T(8,128)(2,1)} %get-tuple-element.514, f32[40,1792]{1,0:T(8,128)S(1)} %fusion.25), kind=kOutput, calls=%fused_computation.6 | convolution fusion | flops 587714560 | bytes 15294464 | tf_op jit(solution)/shard_map/while/body/eval_jaxpr/cond/branch_1_fun/dot_general | solution.py:45
  274.7 9.6 %all-to-all-done = bf16[8,5,2048]{2,1,0:T(8,128)(2,1)S(1)} async-done(((bf16[8,5,2048]{2,1,0:T(8,128)(2,1)}), bf16[8,5,2048]{2,1,0:T(8,128)(2,1)S(1)}, u32[]{:S(2)}, u32[]{:S(2)}) %all-to-all-start) | async-done | bytes 163872 | tf_op jit(solution)/shard_map/while/body/eval_jaxpr/all_to_all | solution.py:68
  287.0 6.1 %collective-permute-done.7 = bf16[3,8,2048]{2,1,0:T(8,128)(2,1)S(1)} collective-permute-done((bf16[3,8,2048]{2,1,0:T(8,128)(2,1)S(1)}, bf16[3,8,2048]{2,1,0:T(8,128)(2,1)S(1)}, u32[]{:S(2)}, u32[]{:S(2)}) %collective-permute-start.7) | collective-permute-done | bytes 98336 | tf_op jit(solution)/shard_map/while/body/eval_jaxpr/ppermute | solution.py:16
  307.3 13.3 %conditional.2 = (bf16[8,5,2048]{2,1,0:T(8,128)(2,1)}) conditional(s32[]{:T(128)} %convert_element_type.142, () %tuple.86, (s32[]{:T(128)}, bf16[8,5,2048]{2,1,0:T(8,128)(2,1)S(1)}, bf16[1,5,2048]{2,1,0:T(8,128)(2,1)S(1)}, s32[]{:T(128)}, bf16[1,5,2048]{2,1,0:T(8,128)(2,1)S(1)}, /*index=5*/s32[]{:T(128)}, bf16[1,5,2048]{2,1,0:T(8,128)(2,1)S(1)}, ...), branch_computations={%region_4.4_spmd, %region_5.5_spmd} | conditional | flops 881315840 | bytes 24428620 | solution.py:67
  312.0 7.8 %convolution_convert_fusion = bf16[40,2048]{1,0:T(8,128)(2,1)S(1)} fusion(bf16[1792,2048]{1,0:T(8,128)(2,1)} %get-tuple-element.515, bf16[40,2048]{1,0:T(8,128)(2,1)S(1)} %reshape.154, bf16[2048,1792]{1,0:T(8,128)(2,1)} %get-tuple-element.514, f32[40,1792]{1,0:T(8,128)S(1)} %fusion.25), kind=kOutput, calls=%fused_computation.6 | convolution fusion | flops 587714560 | bytes 15294464 | tf_op jit(solution)/shard_map/while/body/eval_jaxpr/cond/branch_1_fun/dot_general | solution.py:45
  324.0 9.6 %all-to-all-done = bf16[8,5,2048]{2,1,0:T(8,128)(2,1)S(1)} async-done(((bf16[8,5,2048]{2,1,0:T(8,128)(2,1)}), bf16[8,5,2048]{2,1,0:T(8,128)(2,1)S(1)}, u32[]{:S(2)}, u32[]{:S(2)}) %all-to-all-start) | async-done | bytes 163872 | tf_op jit(solution)/shard_map/while/body/eval_jaxpr/all_to_all | solution.py:68
  356.6 13.3 %conditional.2 = (bf16[8,5,2048]{2,1,0:T(8,128)(2,1)}) conditional(s32[]{:T(128)} %convert_element_type.142, () %tuple.86, (s32[]{:T(128)}, bf16[8,5,2048]{2,1,0:T(8,128)(2,1)S(1)}, bf16[1,5,2048]{2,1,0:T(8,128)(2,1)S(1)}, s32[]{:T(128)}, bf16[1,5,2048]{2,1,0:T(8,128)(2,1)S(1)}, /*index=5*/s32[]{:T(128)}, bf16[1,5,2048]{2,1,0:T(8,128)(2,1)S(1)}, ...), branch_computations={%region_4.4_spmd, %region_5.5_spmd} | conditional | flops 881315840 | bytes 24428620 | solution.py:67
  361.3 7.8 %convolution_convert_fusion = bf16[40,2048]{1,0:T(8,128)(2,1)S(1)} fusion(bf16[1792,2048]{1,0:T(8,128)(2,1)} %get-tuple-element.515, bf16[40,2048]{1,0:T(8,128)(2,1)S(1)} %reshape.154, bf16[2048,1792]{1,0:T(8,128)(2,1)} %get-tuple-element.514, f32[40,1792]{1,0:T(8,128)S(1)} %fusion.25), kind=kOutput, calls=%fused_computation.6 | convolution fusion | flops 587714560 | bytes 15294464 | tf_op jit(solution)/shard_map/while/body/eval_jaxpr/cond/branch_1_fun/dot_general | solution.py:45
  373.3 9.6 %all-to-all-done = bf16[8,5,2048]{2,1,0:T(8,128)(2,1)S(1)} async-done(((bf16[8,5,2048]{2,1,0:T(8,128)(2,1)}), bf16[8,5,2048]{2,1,0:T(8,128)(2,1)S(1)}, u32[]{:S(2)}, u32[]{:S(2)}) %all-to-all-start) | async-done | bytes 163872 | tf_op jit(solution)/shard_map/while/body/eval_jaxpr/all_to_all | solution.py:68
  405.9 13.3 %conditional.2 = (bf16[8,5,2048]{2,1,0:T(8,128)(2,1)}) conditional(s32[]{:T(128)} %convert_element_type.142, () %tuple.86, (s32[]{:T(128)}, bf16[8,5,2048]{2,1,0:T(8,128)(2,1)S(1)}, bf16[1,5,2048]{2,1,0:T(8,128)(2,1)S(1)}, s32[]{:T(128)}, bf16[1,5,2048]{2,1,0:T(8,128)(2,1)S(1)}, /*index=5*/s32[]{:T(128)}, bf16[1,5,2048]{2,1,0:T(8,128)(2,1)S(1)}, ...), branch_computations={%region_4.4_spmd, %region_5.5_spmd} | conditional | flops 881315840 | bytes 24428620 | solution.py:67
  410.6 7.8 %convolution_convert_fusion = bf16[40,2048]{1,0:T(8,128)(2,1)S(1)} fusion(bf16[1792,2048]{1,0:T(8,128)(2,1)} %get-tuple-element.515, bf16[40,2048]{1,0:T(8,128)(2,1)S(1)} %reshape.154, bf16[2048,1792]{1,0:T(8,128)(2,1)} %get-tuple-element.514, f32[40,1792]{1,0:T(8,128)S(1)} %fusion.25), kind=kOutput, calls=%fused_computation.6 | convolution fusion | flops 587714560 | bytes 15294464 | tf_op jit(solution)/shard_map/while/body/eval_jaxpr/cond/branch_1_fun/dot_general | solution.py:45
  422.6 9.6 %all-to-all-done = bf16[8,5,2048]{2,1,0:T(8,128)(2,1)S(1)} async-done(((bf16[8,5,2048]{2,1,0:T(8,128)(2,1)}), bf16[8,5,2048]{2,1,0:T(8,128)(2,1)S(1)}, u32[]{:S(2)}, u32[]{:S(2)}) %all-to-all-start) | async-done | bytes 163872 | tf_op jit(solution)/shard_map/while/body/eval_jaxpr/all_to_all | solution.py:68
  455.2 13.3 %conditional.2 = (bf16[8,5,2048]{2,1,0:T(8,128)(2,1)}) conditional(s32[]{:T(128)} %convert_element_type.142, () %tuple.86, (s32[]{:T(128)}, bf16[8,5,2048]{2,1,0:T(8,128)(2,1)S(1)}, bf16[1,5,2048]{2,1,0:T(8,128)(2,1)S(1)}, s32[]{:T(128)}, bf16[1,5,2048]{2,1,0:T(8,128)(2,1)S(1)}, /*index=5*/s32[]{:T(128)}, bf16[1,5,2048]{2,1,0:T(8,128)(2,1)S(1)}, ...), branch_computations={%region_4.4_spmd, %region_5.5_spmd} | conditional | flops 881315840 | bytes 24428620 | solution.py:67
  459.9 7.8 %convolution_convert_fusion = bf16[40,2048]{1,0:T(8,128)(2,1)S(1)} fusion(bf16[1792,2048]{1,0:T(8,128)(2,1)} %get-tuple-element.515, bf16[40,2048]{1,0:T(8,128)(2,1)S(1)} %reshape.154, bf16[2048,1792]{1,0:T(8,128)(2,1)} %get-tuple-element.514, f32[40,1792]{1,0:T(8,128)S(1)} %fusion.25), kind=kOutput, calls=%fused_computation.6 | convolution fusion | flops 587714560 | bytes 15294464 | tf_op jit(solution)/shard_map/while/body/eval_jaxpr/cond/branch_1_fun/dot_general | solution.py:45
  471.9 9.6 %all-to-all-done = bf16[8,5,2048]{2,1,0:T(8,128)(2,1)S(1)} async-done(((bf16[8,5,2048]{2,1,0:T(8,128)(2,1)}), bf16[8,5,2048]{2,1,0:T(8,128)(2,1)S(1)}, u32[]{:S(2)}, u32[]{:S(2)}) %all-to-all-start) | async-done | bytes 163872 | tf_op jit(solution)/shard_map/while/body/eval_jaxpr/all_to_all | solution.py:68
  484.3 6.1 %collective-permute-done.7 = bf16[3,8,2048]{2,1,0:T(8,128)(2,1)S(1)} collective-permute-done((bf16[3,8,2048]{2,1,0:T(8,128)(2,1)S(1)}, bf16[3,8,2048]{2,1,0:T(8,128)(2,1)S(1)}, u32[]{:S(2)}, u32[]{:S(2)}) %collective-permute-start.7) | collective-permute-done | bytes 98336 | tf_op jit(solution)/shard_map/while/body/eval_jaxpr/ppermute | solution.py:16
  504.5 13.3 %conditional.2 = (bf16[8,5,2048]{2,1,0:T(8,128)(2,1)}) conditional(s32[]{:T(128)} %convert_element_type.142, () %tuple.86, (s32[]{:T(128)}, bf16[8,5,2048]{2,1,0:T(8,128)(2,1)S(1)}, bf16[1,5,2048]{2,1,0:T(8,128)(2,1)S(1)}, s32[]{:T(128)}, bf16[1,5,2048]{2,1,0:T(8,128)(2,1)S(1)}, /*index=5*/s32[]{:T(128)}, bf16[1,5,2048]{2,1,0:T(8,128)(2,1)S(1)}, ...), branch_computations={%region_4.4_spmd, %region_5.5_spmd} | conditional | flops 881315840 | bytes 24428620 | solution.py:67
  509.2 7.8 %convolution_convert_fusion = bf16[40,2048]{1,0:T(8,128)(2,1)S(1)} fusion(bf16[1792,2048]{1,0:T(8,128)(2,1)} %get-tuple-element.515, bf16[40,2048]{1,0:T(8,128)(2,1)S(1)} %reshape.154, bf16[2048,1792]{1,0:T(8,128)(2,1)} %get-tuple-element.514, f32[40,1792]{1,0:T(8,128)S(1)} %fusion.25), kind=kOutput, calls=%fused_computation.6 | convolution fusion | flops 587714560 | bytes 15294464 | tf_op jit(solution)/shard_map/while/body/eval_jaxpr/cond/branch_1_fun/dot_general | solution.py:45
  521.2 9.6 %all-to-all-done = bf16[8,5,2048]{2,1,0:T(8,128)(2,1)S(1)} async-done(((bf16[8,5,2048]{2,1,0:T(8,128)(2,1)}), bf16[8,5,2048]{2,1,0:T(8,128)(2,1)S(1)}, u32[]{:S(2)}, u32[]{:S(2)}) %all-to-all-start) | async-done | bytes 163872 | tf_op jit(solution)/shard_map/while/body/eval_jaxpr/all_to_all | solution.py:68
  (552 shorter events, 313.2 us)
Async XLA Ops:
  5.0 8.2 %collective-permute-start.1 = (bf16[1,5,2048]{2,1,0:T(8,128)(2,1)S(1)}, bf16[1,5,2048]{2,1,0:T(8,128)(2,1)S(1)}, u32[]{:S(2)}, u32[]{:S(2)}) collective-permute-start(bf16[1,5,2048]{2,1,0:T(8,128)(2,1)S(1)} %get-tuple-element.760), channel_id=1, source_target_pairs={{0,2},{1,3},{2,0},{3,1},{4,6},{5,7},{6,4},{7,5},{8,10},{9,11},{10,... | collective-permute-start | bytes 61448 | tf_op jit(solution)/shard_map/while/body/eval_jaxpr/ppermute | solution.py:64
  6.7 6.7 %collective-permute-start.2 = (bf16[1,5,2048]{2,1,0:T(8,128)(2,1)S(1)}, bf16[1,5,2048]{2,1,0:T(8,128)(2,1)S(1)}, u32[]{:S(2)}, u32[]{:S(2)}) collective-permute-start(bf16[1,5,2048]{2,1,0:T(8,128)(2,1)S(1)} %get-tuple-element.761), channel_id=1, source_target_pairs={{0,3},{1,2},{2,1},{3,0},{4,7},{5,6},{6,5},{7,4},{8,11},{9,10},{10,... | collective-permute-start | bytes 61448 | tf_op jit(solution)/shard_map/while/body/eval_jaxpr/ppermute | solution.py:64
  19.1 13.1 %all-to-all-start = ((bf16[8,5,2048]{2,1,0:T(8,128)(2,1)}), bf16[8,5,2048]{2,1,0:T(8,128)(2,1)S(1)}, u32[]{:S(2)}, u32[]{:S(2)}) async-start(bf16[8,5,2048]{2,1,0:T(8,128)(2,1)} %get-tuple-element.857), calls=%async_computation | async-start | bytes 524288 | tf_op jit(solution)/shard_map/while/body/eval_jaxpr/all_to_all | solution.py:68
  33.5 6.5 %collective-permute-start.7 = (bf16[3,8,2048]{2,1,0:T(8,128)(2,1)S(1)}, bf16[3,8,2048]{2,1,0:T(8,128)(2,1)S(1)}, u32[]{:S(2)}, u32[]{:S(2)}) collective-permute-start(bf16[3,8,2048]{2,1,0:T(8,128)(2,1)S(1)} %maximum_select_fusion.2), channel_id=1, source_target_pairs={{0,8},{8,16},{16,24},{1,9},{9,17},{17,25},{2,10},{10,18},{18,26},{... | collective-permute-start | bytes 294920 | tf_op jit(solution)/shard_map/while/body/eval_jaxpr/ppermute | solution.py:16
  42.9 8.0 %collective-permute-start.2 = (bf16[1,5,2048]{2,1,0:T(8,128)(2,1)S(1)}, bf16[1,5,2048]{2,1,0:T(8,128)(2,1)S(1)}, u32[]{:S(2)}, u32[]{:S(2)}) collective-permute-start(bf16[1,5,2048]{2,1,0:T(8,128)(2,1)S(1)} %get-tuple-element.761), channel_id=1, source_target_pairs={{0,3},{1,2},{2,1},{3,0},{4,7},{5,6},{6,5},{7,4},{8,11},{9,10},{10,... | collective-permute-start | bytes 61448 | tf_op jit(solution)/shard_map/while/body/eval_jaxpr/ppermute | solution.py:64
  54.6 13.4 %all-to-all-start = ((bf16[8,5,2048]{2,1,0:T(8,128)(2,1)}), bf16[8,5,2048]{2,1,0:T(8,128)(2,1)S(1)}, u32[]{:S(2)}, u32[]{:S(2)}) async-start(bf16[8,5,2048]{2,1,0:T(8,128)(2,1)} %get-tuple-element.857), calls=%async_computation | async-start | bytes 524288 | tf_op jit(solution)/shard_map/while/body/eval_jaxpr/all_to_all | solution.py:68
  78.7 8.0 %collective-permute-start.2 = (bf16[1,5,2048]{2,1,0:T(8,128)(2,1)S(1)}, bf16[1,5,2048]{2,1,0:T(8,128)(2,1)S(1)}, u32[]{:S(2)}, u32[]{:S(2)}) collective-permute-start(bf16[1,5,2048]{2,1,0:T(8,128)(2,1)S(1)} %get-tuple-element.761), channel_id=1, source_target_pairs={{0,3},{1,2},{2,1},{3,0},{4,7},{5,6},{6,5},{7,4},{8,11},{9,10},{10,... | collective-permute-start | bytes 61448 | tf_op jit(solution)/shard_map/while/body/eval_jaxpr/ppermute | solution.py:64
  90.5 13.4 %all-to-all-start = ((bf16[8,5,2048]{2,1,0:T(8,128)(2,1)}), bf16[8,5,2048]{2,1,0:T(8,128)(2,1)S(1)}, u32[]{:S(2)}, u32[]{:S(2)}) async-start(bf16[8,5,2048]{2,1,0:T(8,128)(2,1)} %get-tuple-element.857), calls=%async_computation | async-start | bytes 524288 | tf_op jit(solution)/shard_map/while/body/eval_jaxpr/all_to_all | solution.py:68
  105.3 39.9 %collective-permute-start.7 = (bf16[3,8,2048]{2,1,0:T(8,128)(2,1)S(1)}, bf16[3,8,2048]{2,1,0:T(8,128)(2,1)S(1)}, u32[]{:S(2)}, u32[]{:S(2)}) collective-permute-start(bf16[3,8,2048]{2,1,0:T(8,128)(2,1)S(1)} %maximum_select_fusion.2), channel_id=1, source_target_pairs={{0,8},{8,16},{16,24},{1,9},{9,17},{17,25},{2,10},{10,18},{18,26},{... | collective-permute-start | bytes 294920 | tf_op jit(solution)/shard_map/while/body/eval_jaxpr/ppermute | solution.py:16
  148.1 8.0 %collective-permute-start.2 = (bf16[1,5,2048]{2,1,0:T(8,128)(2,1)S(1)}, bf16[1,5,2048]{2,1,0:T(8,128)(2,1)S(1)}, u32[]{:S(2)}, u32[]{:S(2)}) collective-permute-start(bf16[1,5,2048]{2,1,0:T(8,128)(2,1)S(1)} %get-tuple-element.761), channel_id=1, source_target_pairs={{0,3},{1,2},{2,1},{3,0},{4,7},{5,6},{6,5},{7,4},{8,11},{9,10},{10,... | collective-permute-start | bytes 61448 | tf_op jit(solution)/shard_map/while/body/eval_jaxpr/ppermute | solution.py:64
  172.6 13.1 %all-to-all-start = ((bf16[8,5,2048]{2,1,0:T(8,128)(2,1)}), bf16[8,5,2048]{2,1,0:T(8,128)(2,1)S(1)}, u32[]{:S(2)}, u32[]{:S(2)}) async-start(bf16[8,5,2048]{2,1,0:T(8,128)(2,1)} %get-tuple-element.857), calls=%async_computation | async-start | bytes 524288 | tf_op jit(solution)/shard_map/while/body/eval_jaxpr/all_to_all | solution.py:68
  187.1 7.4 %collective-permute-start.7 = (bf16[3,8,2048]{2,1,0:T(8,128)(2,1)S(1)}, bf16[3,8,2048]{2,1,0:T(8,128)(2,1)S(1)}, u32[]{:S(2)}, u32[]{:S(2)}) collective-permute-start(bf16[3,8,2048]{2,1,0:T(8,128)(2,1)S(1)} %maximum_select_fusion.2), channel_id=1, source_target_pairs={{0,8},{8,16},{16,24},{1,9},{9,17},{17,25},{2,10},{10,18},{18,26},{... | collective-permute-start | bytes 294920 | tf_op jit(solution)/shard_map/while/body/eval_jaxpr/ppermute | solution.py:16
  197.4 8.0 %collective-permute-start.2 = (bf16[1,5,2048]{2,1,0:T(8,128)(2,1)S(1)}, bf16[1,5,2048]{2,1,0:T(8,128)(2,1)S(1)}, u32[]{:S(2)}, u32[]{:S(2)}) collective-permute-start(bf16[1,5,2048]{2,1,0:T(8,128)(2,1)S(1)} %get-tuple-element.761), channel_id=1, source_target_pairs={{0,3},{1,2},{2,1},{3,0},{4,7},{5,6},{6,5},{7,4},{8,11},{9,10},{10,... | collective-permute-start | bytes 61448 | tf_op jit(solution)/shard_map/while/body/eval_jaxpr/ppermute | solution.py:64
  221.9 13.1 %all-to-all-start = ((bf16[8,5,2048]{2,1,0:T(8,128)(2,1)}), bf16[8,5,2048]{2,1,0:T(8,128)(2,1)S(1)}, u32[]{:S(2)}, u32[]{:S(2)}) async-start(bf16[8,5,2048]{2,1,0:T(8,128)(2,1)} %get-tuple-element.857), calls=%async_computation | async-start | bytes 524288 | tf_op jit(solution)/shard_map/while/body/eval_jaxpr/all_to_all | solution.py:68
  236.4 7.4 %collective-permute-start.7 = (bf16[3,8,2048]{2,1,0:T(8,128)(2,1)S(1)}, bf16[3,8,2048]{2,1,0:T(8,128)(2,1)S(1)}, u32[]{:S(2)}, u32[]{:S(2)}) collective-permute-start(bf16[3,8,2048]{2,1,0:T(8,128)(2,1)S(1)} %maximum_select_fusion.2), channel_id=1, source_target_pairs={{0,8},{8,16},{16,24},{1,9},{9,17},{17,25},{2,10},{10,18},{18,26},{... | collective-permute-start | bytes 294920 | tf_op jit(solution)/shard_map/while/body/eval_jaxpr/ppermute | solution.py:16
  246.7 8.0 %collective-permute-start.2 = (bf16[1,5,2048]{2,1,0:T(8,128)(2,1)S(1)}, bf16[1,5,2048]{2,1,0:T(8,128)(2,1)S(1)}, u32[]{:S(2)}, u32[]{:S(2)}) collective-permute-start(bf16[1,5,2048]{2,1,0:T(8,128)(2,1)S(1)} %get-tuple-element.761), channel_id=1, source_target_pairs={{0,3},{1,2},{2,1},{3,0},{4,7},{5,6},{6,5},{7,4},{8,11},{9,10},{10,... | collective-permute-start | bytes 61448 | tf_op jit(solution)/shard_map/while/body/eval_jaxpr/ppermute | solution.py:64
  271.2 13.1 %all-to-all-start = ((bf16[8,5,2048]{2,1,0:T(8,128)(2,1)}), bf16[8,5,2048]{2,1,0:T(8,128)(2,1)S(1)}, u32[]{:S(2)}, u32[]{:S(2)}) async-start(bf16[8,5,2048]{2,1,0:T(8,128)(2,1)} %get-tuple-element.857), calls=%async_computation | async-start | bytes 524288 | tf_op jit(solution)/shard_map/while/body/eval_jaxpr/all_to_all | solution.py:68
  285.7 7.4 %collective-permute-start.7 = (bf16[3,8,2048]{2,1,0:T(8,128)(2,1)S(1)}, bf16[3,8,2048]{2,1,0:T(8,128)(2,1)S(1)}, u32[]{:S(2)}, u32[]{:S(2)}) collective-permute-start(bf16[3,8,2048]{2,1,0:T(8,128)(2,1)S(1)} %maximum_select_fusion.2), channel_id=1, source_target_pairs={{0,8},{8,16},{16,24},{1,9},{9,17},{17,25},{2,10},{10,18},{18,26},{... | collective-permute-start | bytes 294920 | tf_op jit(solution)/shard_map/while/body/eval_jaxpr/ppermute | solution.py:16
  296.0 8.0 %collective-permute-start.2 = (bf16[1,5,2048]{2,1,0:T(8,128)(2,1)S(1)}, bf16[1,5,2048]{2,1,0:T(8,128)(2,1)S(1)}, u32[]{:S(2)}, u32[]{:S(2)}) collective-permute-start(bf16[1,5,2048]{2,1,0:T(8,128)(2,1)S(1)} %get-tuple-element.761), channel_id=1, source_target_pairs={{0,3},{1,2},{2,1},{3,0},{4,7},{5,6},{6,5},{7,4},{8,11},{9,10},{10,... | collective-permute-start | bytes 61448 | tf_op jit(solution)/shard_map/while/body/eval_jaxpr/ppermute | solution.py:64
  320.5 13.1 %all-to-all-start = ((bf16[8,5,2048]{2,1,0:T(8,128)(2,1)}), bf16[8,5,2048]{2,1,0:T(8,128)(2,1)S(1)}, u32[]{:S(2)}, u32[]{:S(2)}) async-start(bf16[8,5,2048]{2,1,0:T(8,128)(2,1)} %get-tuple-element.857), calls=%async_computation | async-start | bytes 524288 | tf_op jit(solution)/shard_map/while/body/eval_jaxpr/all_to_all | solution.py:68
  335.0 7.4 %collective-permute-start.7 = (bf16[3,8,2048]{2,1,0:T(8,128)(2,1)S(1)}, bf16[3,8,2048]{2,1,0:T(8,128)(2,1)S(1)}, u32[]{:S(2)}, u32[]{:S(2)}) collective-permute-start(bf16[3,8,2048]{2,1,0:T(8,128)(2,1)S(1)} %maximum_select_fusion.2), channel_id=1, source_target_pairs={{0,8},{8,16},{16,24},{1,9},{9,17},{17,25},{2,10},{10,18},{18,26},{... | collective-permute-start | bytes 294920 | tf_op jit(solution)/shard_map/while/body/eval_jaxpr/ppermute | solution.py:16
  345.3 8.0 %collective-permute-start.2 = (bf16[1,5,2048]{2,1,0:T(8,128)(2,1)S(1)}, bf16[1,5,2048]{2,1,0:T(8,128)(2,1)S(1)}, u32[]{:S(2)}, u32[]{:S(2)}) collective-permute-start(bf16[1,5,2048]{2,1,0:T(8,128)(2,1)S(1)} %get-tuple-element.761), channel_id=1, source_target_pairs={{0,3},{1,2},{2,1},{3,0},{4,7},{5,6},{6,5},{7,4},{8,11},{9,10},{10,... | collective-permute-start | bytes 61448 | tf_op jit(solution)/shard_map/while/body/eval_jaxpr/ppermute | solution.py:64
  369.9 13.1 %all-to-all-start = ((bf16[8,5,2048]{2,1,0:T(8,128)(2,1)}), bf16[8,5,2048]{2,1,0:T(8,128)(2,1)S(1)}, u32[]{:S(2)}, u32[]{:S(2)}) async-start(bf16[8,5,2048]{2,1,0:T(8,128)(2,1)} %get-tuple-element.857), calls=%async_computation | async-start | bytes 524288 | tf_op jit(solution)/shard_map/while/body/eval_jaxpr/all_to_all | solution.py:68
  384.3 7.4 %collective-permute-start.7 = (bf16[3,8,2048]{2,1,0:T(8,128)(2,1)S(1)}, bf16[3,8,2048]{2,1,0:T(8,128)(2,1)S(1)}, u32[]{:S(2)}, u32[]{:S(2)}) collective-permute-start(bf16[3,8,2048]{2,1,0:T(8,128)(2,1)S(1)} %maximum_select_fusion.2), channel_id=1, source_target_pairs={{0,8},{8,16},{16,24},{1,9},{9,17},{17,25},{2,10},{10,18},{18,26},{... | collective-permute-start | bytes 294920 | tf_op jit(solution)/shard_map/while/body/eval_jaxpr/ppermute | solution.py:16
  394.6 8.0 %collective-permute-start.2 = (bf16[1,5,2048]{2,1,0:T(8,128)(2,1)S(1)}, bf16[1,5,2048]{2,1,0:T(8,128)(2,1)S(1)}, u32[]{:S(2)}, u32[]{:S(2)}) collective-permute-start(bf16[1,5,2048]{2,1,0:T(8,128)(2,1)S(1)} %get-tuple-element.761), channel_id=1, source_target_pairs={{0,3},{1,2},{2,1},{3,0},{4,7},{5,6},{6,5},{7,4},{8,11},{9,10},{10,... | collective-permute-start | bytes 61448 | tf_op jit(solution)/shard_map/while/body/eval_jaxpr/ppermute | solution.py:64
  419.2 13.1 %all-to-all-start = ((bf16[8,5,2048]{2,1,0:T(8,128)(2,1)}), bf16[8,5,2048]{2,1,0:T(8,128)(2,1)S(1)}, u32[]{:S(2)}, u32[]{:S(2)}) async-start(bf16[8,5,2048]{2,1,0:T(8,128)(2,1)} %get-tuple-element.857), calls=%async_computation | async-start | bytes 524288 | tf_op jit(solution)/shard_map/while/body/eval_jaxpr/all_to_all | solution.py:68
  433.7 7.4 %collective-permute-start.7 = (bf16[3,8,2048]{2,1,0:T(8,128)(2,1)S(1)}, bf16[3,8,2048]{2,1,0:T(8,128)(2,1)S(1)}, u32[]{:S(2)}, u32[]{:S(2)}) collective-permute-start(bf16[3,8,2048]{2,1,0:T(8,128)(2,1)S(1)} %maximum_select_fusion.2), channel_id=1, source_target_pairs={{0,8},{8,16},{16,24},{1,9},{9,17},{17,25},{2,10},{10,18},{18,26},{... | collective-permute-start | bytes 294920 | tf_op jit(solution)/shard_map/while/body/eval_jaxpr/ppermute | solution.py:16
  443.9 8.0 %collective-permute-start.2 = (bf16[1,5,2048]{2,1,0:T(8,128)(2,1)S(1)}, bf16[1,5,2048]{2,1,0:T(8,128)(2,1)S(1)}, u32[]{:S(2)}, u32[]{:S(2)}) collective-permute-start(bf16[1,5,2048]{2,1,0:T(8,128)(2,1)S(1)} %get-tuple-element.761), channel_id=1, source_target_pairs={{0,3},{1,2},{2,1},{3,0},{4,7},{5,6},{6,5},{7,4},{8,11},{9,10},{10,... | collective-permute-start | bytes 61448 | tf_op jit(solution)/shard_map/while/body/eval_jaxpr/ppermute | solution.py:64
  468.5 13.1 %all-to-all-start = ((bf16[8,5,2048]{2,1,0:T(8,128)(2,1)}), bf16[8,5,2048]{2,1,0:T(8,128)(2,1)S(1)}, u32[]{:S(2)}, u32[]{:S(2)}) async-start(bf16[8,5,2048]{2,1,0:T(8,128)(2,1)} %get-tuple-element.857), calls=%async_computation | async-start | bytes 524288 | tf_op jit(solution)/shard_map/while/body/eval_jaxpr/all_to_all | solution.py:68
  483.0 7.4 %collective-permute-start.7 = (bf16[3,8,2048]{2,1,0:T(8,128)(2,1)S(1)}, bf16[3,8,2048]{2,1,0:T(8,128)(2,1)S(1)}, u32[]{:S(2)}, u32[]{:S(2)}) collective-permute-start(bf16[3,8,2048]{2,1,0:T(8,128)(2,1)S(1)} %maximum_select_fusion.2), channel_id=1, source_target_pairs={{0,8},{8,16},{16,24},{1,9},{9,17},{17,25},{2,10},{10,18},{18,26},{... | collective-permute-start | bytes 294920 | tf_op jit(solution)/shard_map/while/body/eval_jaxpr/ppermute | solution.py:16
  493.2 8.0 %collective-permute-start.2 = (bf16[1,5,2048]{2,1,0:T(8,128)(2,1)S(1)}, bf16[1,5,2048]{2,1,0:T(8,128)(2,1)S(1)}, u32[]{:S(2)}, u32[]{:S(2)}) collective-permute-start(bf16[1,5,2048]{2,1,0:T(8,128)(2,1)S(1)} %get-tuple-element.761), channel_id=1, source_target_pairs={{0,3},{1,2},{2,1},{3,0},{4,7},{5,6},{6,5},{7,4},{8,11},{9,10},{10,... | collective-permute-start | bytes 61448 | tf_op jit(solution)/shard_map/while/body/eval_jaxpr/ppermute | solution.py:64
  517.8 13.1 %all-to-all-start = ((bf16[8,5,2048]{2,1,0:T(8,128)(2,1)}), bf16[8,5,2048]{2,1,0:T(8,128)(2,1)S(1)}, u32[]{:S(2)}, u32[]{:S(2)}) async-start(bf16[8,5,2048]{2,1,0:T(8,128)(2,1)} %get-tuple-element.857), calls=%async_computation | async-start | bytes 524288 | tf_op jit(solution)/shard_map/while/body/eval_jaxpr/all_to_all | solution.py:68
  (69 other events, 381.5 us)
